TPU v7x, 32 devices: a whole 2x2x4 slice. The times are simulated.
32 devices in a mesh: chan: 4 (over z), pulse: 4 (over x, core), range: 2 (over y).
Axes of the slice: x: 2, y: 2, z: 4, core: 2. Of those that a mesh axis runs over, the one named last changes fastest.
Arguments:
- signal: bfloat16 [2, 64, 32, 8192], P(None, 'chan', 'pulse', 'range'), may hold values from -6 to 6
- steering: bfloat16 [2, 32, 64], replicated, may hold values from -0.5 to 0.5
- spectrum: float32 [2, 8192], replicated, may hold values from -6 to 6
Outputs:
- detection: float32 [32, 32, 8192], P('chan', 'pulse', 'range')
All inputs are finite; a program needn't handle non-finite values.
Results may differ from a plain program's by a relative error of at most 0.0087.
Values may be sent and summed in bfloat16 or wider, within the bound.
A program may use at most 64 MiB of HBM per device.

v0:
```python
import math
import jax
import jax.numpy as jnp
from jax import lax
from jax.sharding import PartitionSpec as P

GUARD = 4
TRAIN = 16
PRECISE = lax.Precision.HIGHEST
NOISE_FLOOR = 0.25


def padded_2(x, sides, width):
    for axis, dim in sides:
        peers, length = (lax.axis_size(axis), x.shape[dim])
        up = [(i, (i + 1) % peers) for i in range(peers - 1)]
        down = [(j, i) for i, j in up]
        last = lax.slice_in_dim(x, length - width, length, axis=dim)
        initial = lax.slice_in_dim(x, 0, width, axis=dim)
        before = lax.ppermute(last, axis, up)
        after = lax.ppermute(initial, axis, down)
        x = jnp.concatenate([before, x, after], axis=dim)
    return x


def doppler_tables(pulse_count):
    row_ids = lax.broadcasted_iota(jnp.int32, (pulse_count, pulse_count), 0)
    col_ids = lax.broadcasted_iota(jnp.int32, (pulse_count, pulse_count), 1)
    phase_angle = (row_ids * col_ids % pulse_count).astype(jnp.float32) * (
        2.0 * math.pi / pulse_count
    )
    norm_scale = 1.0 / math.sqrt(pulse_count)
    table_real = (jnp.cos(phase_angle) * norm_scale).astype(jnp.bfloat16)
    table_imag = (-jnp.sin(phase_angle) * norm_scale).astype(jnp.bfloat16)
    return (table_real, table_imag)


def phase_table(row_count, col_count, period_len, direction):
    row_ids = lax.broadcasted_iota(jnp.int32, (row_count, col_count), 0)
    col_ids = lax.broadcasted_iota(jnp.int32, (row_count, col_count), 1)
    phase_angle = (row_ids * col_ids % period_len).astype(jnp.float32) * (
        2.0 * math.pi / period_len
    )
    return (jnp.cos(phase_angle), direction * jnp.sin(phase_angle))


def rotate_by(field_pair, table_pair):
    return (
        field_pair[0] * table_pair[0] - field_pair[1] * table_pair[1],
        field_pair[0] * table_pair[1] + field_pair[1] * table_pair[0],
    )


def mix_blocks(table_pair, field_pair):

    def contract(table_part, field_part):
        return jnp.einsum("km,bpmn->bpkn", table_part, field_part, precision=PRECISE)

    return (
        contract(table_pair[0], field_pair[0]) - contract(table_pair[1], field_pair[1]),
        contract(table_pair[0], field_pair[1]) + contract(table_pair[1], field_pair[0]),
    )


def mix_lanes(field_pair, table_pair):

    def contract(field_part, table_part):
        return jnp.einsum("bpkm,mn->bpkn", field_part, table_part, precision=PRECISE)

    return (
        contract(field_pair[0], table_pair[0]) - contract(field_pair[1], table_pair[1]),
        contract(field_pair[0], table_pair[1]) + contract(field_pair[1], table_pair[0]),
    )


def local_transform(field_pair, direction):
    size_all = field_pair[0].shape[-1]
    blocks = size_all // 128
    leading = field_pair[0].shape[:-1]
    shaped = tuple((member.reshape(leading + (blocks, 128)) for member in field_pair))
    outer_table = phase_table(blocks, blocks, blocks, direction)
    twiddle = phase_table(blocks, 128, size_all, direction)
    inner_table = phase_table(128, 128, 128, direction)
    if direction < 0:
        shaped = mix_blocks(outer_table, shaped)
        shaped = rotate_by(shaped, twiddle)
        shaped = mix_lanes(shaped, inner_table)
    else:
        shaped = mix_lanes(shaped, inner_table)
        shaped = rotate_by(shaped, twiddle)
        shaped = mix_blocks(outer_table, shaped)
    return tuple((member.reshape(leading + (size_all,)) for member in shaped))


def stack_weights(w_real, w_imag):
    return jnp.concatenate(
        [jnp.concatenate([w_real, -w_imag], 1), jnp.concatenate([w_imag, w_real], 1)], 0
    )


def shards(signal, steering, spectrum):
    beam_count = steering.shape[1]
    chan_count = steering.shape[2]
    pulse_local = signal.shape[2]
    gate_count = signal.shape[3]
    stacked = stack_weights(steering[0], steering[1])
    samples = lax.all_to_all(signal, "chan", split_axis=2, concat_axis=1, tiled=True)
    pulses_here = samples.shape[2]
    gates_here = samples.shape[3]
    flat_samples = samples.reshape(2 * chan_count, pulses_here * gates_here)
    formed = jnp.dot(stacked, flat_samples, preferred_element_type=jnp.float32)
    formed = formed.astype(jnp.bfloat16).reshape(2, beam_count, pulses_here, gates_here)
    beam_data = lax.all_to_all(formed, "chan", split_axis=1, concat_axis=2, tiled=True)
    beam_local = beam_data.shape[1]
    range_count = lax.axis_size("range")
    range_index = lax.axis_index("range")
    full_length = gate_count * range_count
    inverse_scale = 1.0 / full_length
    shard_piece = lax.all_gather(beam_data, "range", axis=3, tiled=True)
    shard_count = shard_piece.shape[3] // gate_count
    members = shard_piece.astype(jnp.float32).reshape(
        2, beam_local, pulse_local, shard_count, gate_count
    )
    source = jnp.arange(shard_count, dtype=jnp.int32)
    phase_angle = (source * range_index % range_count).astype(jnp.float32) * (
        2.0 * math.pi / range_count
    )
    cos_part = jnp.cos(phase_angle)[:, None]
    sin_part = -jnp.sin(phase_angle)[:, None]
    sum_real = jnp.sum(members[0] * cos_part - members[1] * sin_part, axis=2)
    sum_imag = jnp.sum(members[0] * sin_part + members[1] * cos_part, axis=2)
    folded = (sum_real, sum_imag)
    gate_ids = lax.broadcasted_iota(jnp.int32, (gate_count,), 0)
    global_angle = (gate_ids * range_index % full_length).astype(jnp.float32) * (
        2.0 * math.pi / full_length
    )
    folded = rotate_by(folded, (jnp.cos(global_angle), -jnp.sin(global_angle)))
    spectrum_local = local_transform(folded, -1.0)
    response = spectrum.reshape(2, gate_count, range_count)
    response = lax.dynamic_index_in_dim(response, range_index, axis=2, keepdims=False)
    response = jnp.transpose(response.reshape(2, 128, gate_count // 128), (0, 2, 1)).reshape(
        2, gate_count
    )
    filtered = rotate_by(spectrum_local, (response[0], response[1]))
    restored = local_transform(filtered, 1.0)
    restored = rotate_by(restored, (jnp.cos(global_angle), jnp.sin(global_angle)))
    shard_piece = (
        lax.all_gather(restored[0], "range", axis=2, tiled=True),
        lax.all_gather(restored[1], "range", axis=2, tiled=True),
    )
    shard_count = shard_piece[0].shape[2] // gate_count
    rows_real = shard_piece[0].reshape(beam_local, pulse_local, shard_count, gate_count)
    rows_imag = shard_piece[1].reshape(beam_local, pulse_local, shard_count, gate_count)
    source = jnp.arange(shard_count, dtype=jnp.int32)
    phase_angle = (source * range_index % range_count).astype(jnp.float32) * (
        2.0 * math.pi / range_count
    )
    cos_part = jnp.cos(phase_angle)[:, None]
    sin_part = jnp.sin(phase_angle)[:, None]
    sum_real = jnp.sum(rows_real * cos_part - rows_imag * sin_part, axis=2)
    sum_imag = jnp.sum(rows_real * sin_part + rows_imag * cos_part, axis=2)
    compressed = jnp.stack([sum_real * inverse_scale, sum_imag * inverse_scale]).astype(
        jnp.bfloat16
    )
    pulse_total = pulse_local * lax.axis_size("pulse")
    dop_real, dop_imag = doppler_tables(pulse_total)
    columns = lax.all_to_all(compressed, "pulse", split_axis=3, concat_axis=2, tiled=True)

    def product(table_part, values):
        return jnp.einsum("fp,bpr->bfr", table_part, values, preferred_element_type=jnp.float32)

    mixed_real = product(dop_real, columns[0]) - product(dop_imag, columns[1])
    mixed_imag = product(dop_real, columns[1]) + product(dop_imag, columns[0])
    power_part = lax.all_to_all(
        mixed_real * mixed_real + mixed_imag * mixed_imag,
        "pulse",
        split_axis=1,
        concat_axis=2,
        tiled=True,
    )
    halo_width = GUARD + TRAIN
    padded = padded_2(power_part, (("range", 2),), halo_width)
    window_sum = jnp.zeros_like(power_part)
    for offset in range(1, TRAIN + 1):
        left_start = halo_width - GUARD - offset
        right_start = halo_width + GUARD + offset
        window_sum = (
            window_sum
            + padded[:, :, left_start : left_start + gate_count]
            + padded[:, :, right_start : right_start + gate_count]
        )
    noise_level = window_sum / (2.0 * TRAIN)
    return power_part / (noise_level + NOISE_FLOOR)


def solution(mesh):
    in_specs = (P(None, "chan", "pulse", "range"), P(), P())
    out_specs = P("chan", "pulse", "range")
    return jax.shard_map(shards, mesh=mesh, in_specs=in_specs, out_specs=out_specs, check_vma=False)
```

profile of v0, /device:TPU:0, one launch (start us, length us, event | category | flops | bytes accessed | tf_op | source)
XLA Modules:
  0.0 388.4 jit_solution(4963313028370823325)
XLA Ops:
  6.5 4.1 %copy.81 = bf16[2,16,8,4096]{3,1,0,2:T(8,128)(2,1)} copy(bf16[2,16,8,4096]{3,2,1,0:T(8,128)(2,1)} %param.3) | data formatting | bytes 4194304 | tf_op args[0]
  10.6 6.5 %all-to-all-start = ((bf16[2,16,8,4096]{3,1,0,2:T(8,128)(2,1)}), bf16[2,16,8,4096]{3,1,0,2:T(8,128)(2,1)S(1)}, u32[]{:S(2)}, u32[]{:S(2)}) async-start(bf16[2,16,8,4096]{3,1,0,2:T(8,128)(2,1)} %copy.81), calls=%async_computation | async-start | bytes 4194304 | tf_op jit(solution)/shard_map/all_to_all | solution.py:107
  17.1 48.2 %all-to-all-done = bf16[2,16,8,4096]{3,1,0,2:T(8,128)(2,1)S(1)} async-done(((bf16[2,16,8,4096]{3,1,0,2:T(8,128)(2,1)}), bf16[2,16,8,4096]{3,1,0,2:T(8,128)(2,1)S(1)}, u32[]{:S(2)}, u32[]{:S(2)}) %all-to-all-start) | async-done | bytes 2097184 | tf_op jit(solution)/shard_map/all_to_all | solution.py:107
  65.3 2.2 copy.82
  67.5 1.3 copy.126
  68.8 0.5 convolution_convert_fusion
  69.3 0.8 reshape.187
  70.1 0.9 copy.83
  71.0 27.7 %all_to_all.66 = bf16[2,32,2,4096]{3,2,0,1:T(2,128)(2,1)S(1)} all-to-all(bf16[2,32,2,4096]{3,2,0,1:T(2,128)(2,1)S(1)} %copy.83), channel_id=1, replica_groups=mesh['chan'=4,'pulse'=4,'range'=2] {'chan'}, dimensions={1} | all-to-all | bytes 2097152 | tf_op jit(solution)/shard_map/all_to_all | solution.py:113
  98.7 0.6 copy.158
  99.3 1.0 copy.85
  100.4 0.3 all-gather.6.cloned.1.call-start
  100.6 6.4 %reshape.188 = f32[2,4096,2]{2,1,0:T(8,128)} reshape(f32[2,8192]{1,0:T(2,128)S(1)} %copy-done.1) | data formatting | bytes 131072 | tf_op jit(solution)/shard_map/reshape | solution.py:139
  107.0 4.7 %dynamic-slice_reduce_fusion = f32[2,4096]{1,0:T(2,128)S(1)} fusion(f32[2,4096,2]{2,1,0:T(8,128)} %reshape.188, s32[]{:T(128)S(6)} %select_n.134), kind=kLoop, calls=%fused_computation.31 | loop fusion | bytes 65540 | tf_op jit(solution)/shard_map/jit(dynamic_index_in_dim)/dynamic_slice | solution.py:140
  111.8 0.1 reshape.189
  112.5 20.2 %all-gather.4.cloned.1.call-done = bf16[2,8,8,8192]{3,1,2,0:T(8,128)(2,1)} async-done(((bf16[2,8,8,4096]{3,1,2,0:T(8,128)(2,1)}), bf16[2,8,8,8192]{3,1,2,0:T(8,128)(2,1)}) %all-gather.4.cloned.1.call-update) | async-done | bytes 2097168 | tf_op jit(solution)/shard_map/all_gather | solution.py:119
  132.7 3.9 %fusion.271 = (f32[1,8,8,8192]{3,1,2,0:T(8,128)}, f32[1,8,8,8192]{3,1,2,0:T(8,128)}) fusion(bf16[2,8,8,8192]{3,1,2,0:T(8,128)(2,1)} %all-gather.4.cloned.1.call-done), kind=kLoop, calls=%fused_computation.365 | loop fusion | bytes 8388608 | tf_op jit(solution)/shard_map/slice | solution.py:130
  136.6 3.0 reshape.202
  139.7 4.4 %reshape.203 = f32[8,8,2,4096]{3,2,0,1:T(2,128)} reshape(f32[1,8,8,8192]{3,1,2,0:T(8,128)} %get-tuple-element.12) | data formatting | bytes 4194304 | tf_op jit(solution)/shard_map/squeeze | solution.py:130
  144.1 5.8 %subtract_reduce_fusion.1 = (f32[8,8,4096]{2,1,0:T(8,128)S(1)}, f32[8,8,4096]{2,1,0:T(8,128)S(1)}) fusion(f32[8,8,2,4096]{3,2,0,1:T(2,128)} %reshape.203, f32[8,8,2,4096]{3,2,0,1:T(2,128)S(1)} %reshape.202, f32[2]{0:T(128)S(1)} %get-tuple-element.24, f32[2]{0:T(128)S(1)} %get-tuple-element.23), kind=kLoop, calls=%fused_computation.35 | loop fusion | flops 3670016 | bytes 6291472 | tf_op jit(solution)/shard_map/reduce_sum | solution.py:130
  149.8 0.6 copy.157
  150.5 0.6 copy.156
  151.1 1.5 fusion.85
  152.6 1.5 fusion.84
  154.1 1.5 fusion.2
  155.6 1.5 fusion.3
  157.1 1.4 fusion.78
  158.5 1.2 fusion.79
  159.8 1.2 convolution_add_fusion.2
  161.0 1.2 convolution_subtract_fusion.2
  162.2 1.2 fusion.80
  163.5 1.2 fusion.81
  164.7 1.2 convolution_add_fusion.1
  165.9 1.2 convolution_subtract_fusion.1
  167.2 1.2 fusion.83
  168.4 1.4 fusion.82
  169.8 2.2 fusion
  172.0 2.4 reshape.191
  174.3 2.2 fusion.1
  176.5 1.5 reshape.190
  178.1 1.6 multiply_subtract_fusion
  179.7 0.7 all-gather.8.cloned.1.call-update
  180.4 32.5 %all-gather.6.cloned.1.call-done = f32[8,8,8192]{2,1,0:T(8,128)} async-done(((f32[8,8,4096]{2,1,0:T(8,128)}), f32[8,8,8192]{2,1,0:T(8,128)}) %all-gather.6.cloned.1.call-update) | async-done | bytes 2097168 | tf_op jit(solution)/shard_map/all_gather | solution.py:148
  212.9 34.7 %all-gather.8.cloned.1.call-done = f32[8,8,8192]{2,1,0:T(8,128)} async-done(((f32[8,8,4096]{2,1,0:T(8,128)}), f32[8,8,8192]{2,1,0:T(8,128)}) %all-gather.8.cloned.1.call-update) | async-done | bytes 2097168 | tf_op jit(solution)/shard_map/all_gather | solution.py:149
  247.6 3.2 subtract_reduce_fusion
  250.7 0.6 fusion.74
  251.3 0.6 fusion.75
  252.1 14.0 %copy.106 = bf16[2,8,8,4096]{2,1,0,3:T(8,128)(2,1)} copy(bf16[2,8,8,4096]{3,1,2,0:T(8,128)(2,1)S(1)} %pad_maximum_fusion.2) | data formatting | bytes 2097152 | tf_op jit(solution)/shard_map/stack | solution.py:162
  266.1 20.5 %reshape.205 = bf16[4,2,65536]{2,1,0:T(2,128)(2,1)S(1)} reshape(bf16[4096,2,8,8]{3,2,1,0:T(8,128)(2,1)} %bitcast.133) | data formatting | bytes 2097152
  286.6 17.2 %all_to_all.67 = bf16[4,2,65536]{2,1,0:T(2,128)(2,1)S(1)} all-to-all(bf16[4,2,65536]{2,1,0:T(2,128)(2,1)S(1)} %reshape.205), channel_id=1, replica_groups=mesh['chan'=4,'pulse'=4,'range'=2] {'pulse'}, dimensions={0} | all-to-all | bytes 2097152 | tf_op jit(solution)/shard_map/all_to_all | solution.py:167
  303.8 21.7 %reshape.206 = bf16[4096,2,8,8]{3,2,1,0:T(8,128)(2,1)} reshape(bf16[4,2,65536]{2,1,0:T(2,128)(2,1)S(1)} %all_to_all.67) | data formatting | bytes 2097152
  325.5 16.0 %copy.107 = bf16[2,8,8,4,1024]{4,2,3,1,0:T(8,128)(2,1)S(1)} copy(bf16[2,8,8,4,1024]{2,1,0,4,3:T(8,128)(2,1)} %bitcast.134) | data formatting | bytes 2097152 | tf_op jit(solution)/shard_map/all_to_all | solution.py:167
  341.5 0.4 fusion.76
  341.9 0.4 fusion.77
  342.3 0.4 fusion.7
  342.7 0.4 fusion.6
  343.0 0.6 copy.108
  343.6 16.9 %all_to_all.68 = f32[8,32,1024]{2,0,1:T(8,128)S(1)} all-to-all(f32[8,32,1024]{2,0,1:T(8,128)S(1)} %copy.108), channel_id=1, replica_groups=mesh['chan'=4,'pulse'=4,'range'=2] {'pulse'}, dimensions={1} | all-to-all | bytes 2097152 | tf_op jit(solution)/shard_map/all_to_all | solution.py:174
  360.5 0.6 copy.109
  361.2 2.4 collective-permute-start
  363.6 1.3 collective-permute-start.1
  364.9 0.3 collective-permute-done
  365.2 4.2 %collective-permute-done.1 = f32[8,8,20]{2,1,0:T(8,128)S(1)} collective-permute-done((f32[8,8,20]{2,1,0:T(8,128)S(1)}, f32[8,8,20]{2,1,0:T(8,128)S(1)}, u32[]{:S(2)}, u32[]{:S(2)}) %collective-permute-start.1) | collective-permute-done | bytes 5152 | tf_op jit(solution)/shard_map/ppermute | solution.py:21
  369.4 12.0 %fusion.14 = f32[8,8,4096]{2,1,0:T(8,128)} fusion(f32[8,8,4096]{2,1,0:T(8,128)S(1)} %bitcast.151, f32[8,8,20]{2,1,0:T(8,128)S(1)} %collective-permute-done.1, f32[8,8,20]{2,1,0:T(8,128)S(1)} %collective-permute-done), kind=kLoop, calls=%fused_computation.60 | loop fusion | flops 17301504 | bytes 2107392 | tf_op jit(solution)/shard_map/div | solution.py:193
  (23 shorter events, 0.9 us)
Async XLA Ops:
  10.6 6.5 %copy-start.2 = (bf16[2,32,64]{2,1,0:T(8,128)(2,1)S(1)}, bf16[2,32,64]{2,1,0:T(8,128)(2,1)}, u32[]{:S(2)}) copy-start(bf16[2,32,64]{2,1,0:T(8,128)(2,1)} %param.4) | copy-start | bytes 24580
  10.6 54.7 %all-to-all-start = ((bf16[2,16,8,4096]{3,1,0,2:T(8,128)(2,1)}), bf16[2,16,8,4096]{3,1,0,2:T(8,128)(2,1)S(1)}, u32[]{:S(2)}, u32[]{:S(2)}) async-start(bf16[2,16,8,4096]{3,1,0,2:T(8,128)(2,1)} %copy.81), calls=%async_computation | async-start | bytes 4194304 | tf_op jit(solution)/shard_map/all_to_all | solution.py:107
  17.1 115.6 %all-gather.4.cloned.1.call-start = ((), (), s32[]{:S(2)}) async-start(), calls=%async_computation.4 | async-start | bytes 3145728 | tf_op jit(solution)/shard_map/all_gather | solution.py:119
  99.3 1.3 copy-start.1
  100.4 112.5 %all-gather.6.cloned.1.call-start = ((), (), s32[]{:S(2)}) async-start(), calls=%async_computation.5 | async-start | bytes 3145728 | tf_op jit(solution)/shard_map/all_gather | solution.py:148
  176.5 1.5 copy-start
  179.7 67.9 %all-gather.8.cloned.1.call-start = ((), (), s32[]{:S(2)}) async-start(), calls=%async_computation.6 | async-start | bytes 3145728 | tf_op jit(solution)/shard_map/all_gather | solution.py:149
  361.2 4.0 %collective-permute-start = (f32[8,8,20]{2,1,0:T(8,128)S(1)}, f32[8,8,20]{2,1,0:T(8,128)S(1)}, u32[]{:S(2)}, u32[]{:S(2)}) collective-permute-start(f32[8,8,20]{2,1,0:T(8,128)S(1)} %get-tuple-element.13), channel_id=1, source_target_pairs={{0,1},{2,3},{4,5},{6,7},{8,9},{10,11},{12,13},{14,15},{16,17},{18,... | collective-permute-start | bytes 15368 | tf_op jit(solution)/shard_map/ppermute | solution.py:20
  363.6 5.8 %collective-permute-start.1 = (f32[8,8,20]{2,1,0:T(8,128)S(1)}, f32[8,8,20]{2,1,0:T(8,128)S(1)}, u32[]{:S(2)}, u32[]{:S(2)}) collective-permute-start(f32[8,8,20]{2,1,0:T(8,128)S(1)} %get-tuple-element.14), channel_id=1, source_target_pairs={{1,0},{3,2},{5,4},{7,6},{9,8},{11,10},{13,12},{15,14},{17,16},{19,... | collective-permute-start | bytes 15368 | tf_op jit(solution)/shard_map/ppermute | solution.py:21
Sparse Core Ops, SparseCore 0:
  100.5 32.1 all-gather.3
  179.8 33.0 all-gather.5
  214.5 33.0 all-gather.7
where the time goes:
time: 395 us; the launch traced here: 388 us
  waiting for transfers between devices  141 us (36%)
  local copies, waits for them, and re-layouts  112 us (28%)
  blocking collectives  61.8 us (16%)
  matrix products  24.9 us (6%)
  other arithmetic  24.3 us (6%)
  between operations  13.9 us (4%)
  starting transfers between devices  10.5 us (3%)
    unnamed x12, local copies, waits for them, and re-layouts  48.9 us
    all_to_all x1, waiting for transfers between devices, shards(): lax.all_to_all(signal, 'chan', split_axis=2, concat_axis=1, tiled=True)  48.2 us
    all_gather x1, waiting for transfers between devices, shards(): lax.all_gather(restored[1], 'range', axis=2, tiled=True)  34.7 us
    all_gather x1, waiting for transfers between devices, shards(): lax.all_gather(restored[0], 'range', axis=2, tiled=True)  32.5 us
    all_to_all x1, blocking collectives, shards(): lax.all_to_all(formed, 'chan', split_axis=1, concat_axis=2, tiled=True)  27.7 us
    all_gather x1, waiting for transfers between devices, shards(): shard_piece = lax.all_gather(beam_data, 'range', axis=3, tiled=True)  20.2 us
    all_to_all x1, blocking collectives, shards(): lax.all_to_all(compressed, 'pulse', split_axis=3, concat_axis=2, tiled=True)  17.2 us
    all_to_all x1, blocking collectives, shards(): lax.all_to_all(mixed_real * mixed_real + mixed_imag * mixed_imag, 'pulse'...  16.9 us
  transfers between devices with their start and end apart: 6, of which 6 were waited for; matrix products, arithmetic and copies ran while one was open for 3% of the time, Pallas kernels for 0%

commit v1 on v0

--- a/solution.py
+++ b/solution.py
@@ -164,7 +164,10 @@
     )
     pulse_total = pulse_local * lax.axis_size("pulse")
     dop_real, dop_imag = doppler_tables(pulse_total)
-    columns = lax.all_to_all(compressed, "pulse", split_axis=3, concat_axis=2, tiled=True)
+    size = lax.axis_size("pulse")
+    pieces = jnp.stack(jnp.split(compressed, size, axis=3), axis=0)
+    pieces = lax.all_to_all(pieces, "pulse", split_axis=0, concat_axis=0)
+    columns = jnp.concatenate(pieces, axis=2)
 
     def product(table_part, values):
         return jnp.einsum("fp,bpr->bfr", table_part, values, preferred_element_type=jnp.float32)

time: 395 us -> 323 us (0.82)
  local copies, waits for them, and re-layouts: 112 us -> 40.5 us
    unnamed x12 -> x10, local copies, waits for them, and re-layouts: 48.9 us -> 6.64 us
    all_to_all x1 -> x0, local copies, waits for them, and re-layouts: 16 us -> none  [shards(): lax.all_to_all(compressed, 'pulse', split_axis=3, concat_axis=2, tiled=True)]
    another operation x1, local copies, waits for them, and re-layouts: 14 us -> 0.6 us  [shards(): pieces = jnp.stack(jnp.split(compressed, size, axis=3), axis=0)]
  transfers between devices with their start and end apart: 6 -> 6, of which waited for: 6 -> 6; matrix products, arithmetic and copies ran while one was open for 3% -> 4% of each run, Pallas kernels for 0% -> 0%
where the time goes in v1:
time: 323 us; the launch traced here: 317 us
  waiting for transfers between devices  141 us (44%)
  blocking collectives  61.5 us (19%)
  local copies, waits for them, and re-layouts  40.5 us (13%)
  matrix products  25.1 us (8%)
  other arithmetic  24.6 us (8%)
  between operations  13.7 us (4%)
  starting transfers between devices  10.4 us (3%)
    all_to_all x1, waiting for transfers between devices, shards(): lax.all_to_all(signal, 'chan', split_axis=2, concat_axis=1, tiled=True)  48.2 us
    all_gather x1, waiting for transfers between devices, shards(): lax.all_gather(restored[1], 'range', axis=2, tiled=True)  34.7 us
    all_gather x1, waiting for transfers between devices, shards(): lax.all_gather(restored[0], 'range', axis=2, tiled=True)  32.5 us
    all_to_all x1, blocking collectives, shards(): lax.all_to_all(formed, 'chan', split_axis=1, concat_axis=2, tiled=True)  27.7 us
    all_gather x1, waiting for transfers between devices, shards(): shard_piece = lax.all_gather(beam_data, 'range', axis=3, tiled=True)  20.3 us
    all_to_all x1, blocking collectives, shards(): pieces = lax.all_to_all(pieces, 'pulse', split_axis=0, concat_axis=0)  17 us
    all_to_all x1, blocking collectives, shards(): lax.all_to_all(mixed_real * mixed_real + mixed_imag * mixed_imag, 'pulse'...  16.9 us
    dot_general x8, matrix products, contract(): jnp.einsum('km,bpmn->bpkn', table_part, field_part, precision=PRECISE)  12.9 us
  transfers between devices with their start and end apart: 6, of which 6 were waited for; matrix products, arithmetic and copies ran while one was open for 4% of the time, Pallas kernels for 0%

profile of v1, /device:TPU:0, one launch (start us, length us, event | category | flops | bytes accessed | tf_op | source)
XLA Modules:
  0.0 316.7 jit_solution(8438806571566218374)
XLA Ops:
  6.5 4.1 %copy.93 = bf16[2,16,8,4096]{3,1,0,2:T(8,128)(2,1)} copy(bf16[2,16,8,4096]{3,2,1,0:T(8,128)(2,1)} %param.3) | data formatting | bytes 4194304 | tf_op args[0]
  10.6 6.5 %all-to-all-start = ((bf16[2,16,8,4096]{3,1,0,2:T(8,128)(2,1)}), bf16[2,16,8,4096]{3,1,0,2:T(8,128)(2,1)S(1)}, u32[]{:S(2)}, u32[]{:S(2)}) async-start(bf16[2,16,8,4096]{3,1,0,2:T(8,128)(2,1)} %copy.93), calls=%async_computation | async-start | bytes 4194304 | tf_op jit(solution)/shard_map/all_to_all | solution.py:107
  17.1 48.2 %all-to-all-done = bf16[2,16,8,4096]{3,1,0,2:T(8,128)(2,1)S(1)} async-done(((bf16[2,16,8,4096]{3,1,0,2:T(8,128)(2,1)}), bf16[2,16,8,4096]{3,1,0,2:T(8,128)(2,1)S(1)}, u32[]{:S(2)}, u32[]{:S(2)}) %all-to-all-start) | async-done | bytes 2097184 | tf_op jit(solution)/shard_map/all_to_all | solution.py:107
  65.3 2.2 copy.94
  67.5 1.3 copy.139
  68.8 0.5 convolution_convert_fusion
  69.3 0.8 reshape.191
  70.1 0.9 copy.95
  71.0 27.7 %all_to_all.56 = bf16[2,32,2,4096]{3,2,0,1:T(2,128)(2,1)S(1)} all-to-all(bf16[2,32,2,4096]{3,2,0,1:T(2,128)(2,1)S(1)} %copy.95), channel_id=1, replica_groups=mesh['chan'=4,'pulse'=4,'range'=2] {'chan'}, dimensions={1} | all-to-all | bytes 2097152 | tf_op jit(solution)/shard_map/all_to_all | solution.py:113
  98.7 0.6 copy.187
  99.3 1.0 copy.97
  100.4 0.2 all-gather.6.cloned.1.call-start
  100.6 6.4 %reshape.192 = f32[2,4096,2]{2,1,0:T(8,128)} reshape(f32[2,8192]{1,0:T(2,128)S(1)} %copy-done.1) | data formatting | bytes 131072 | tf_op jit(solution)/shard_map/reshape | solution.py:139
  107.0 4.7 %dynamic-slice_reduce_fusion = f32[2,4096]{1,0:T(2,128)S(1)} fusion(f32[2,4096,2]{2,1,0:T(8,128)} %reshape.192, s32[]{:T(128)S(6)} %select_n.134), kind=kLoop, calls=%fused_computation.31 | loop fusion | bytes 65540 | tf_op jit(solution)/shard_map/jit(dynamic_index_in_dim)/dynamic_slice | solution.py:140
  111.7 0.1 reshape.193
  112.2 0.1 sine_negate_fusion
  112.4 20.3 %all-gather.4.cloned.1.call-done = bf16[2,8,8,8192]{3,1,2,0:T(8,128)(2,1)} async-done(((bf16[2,8,8,4096]{3,1,2,0:T(8,128)(2,1)}), bf16[2,8,8,8192]{3,1,2,0:T(8,128)(2,1)}) %all-gather.4.cloned.1.call-update) | async-done | bytes 2097168 | tf_op jit(solution)/shard_map/all_gather | solution.py:119
  132.7 3.9 %fusion.286 = (f32[1,8,8,8192]{3,1,2,0:T(8,128)}, f32[1,8,8,8192]{3,1,2,0:T(8,128)}) fusion(bf16[2,8,8,8192]{3,1,2,0:T(8,128)(2,1)} %all-gather.4.cloned.1.call-done), kind=kLoop, calls=%fused_computation.385 | loop fusion | bytes 8388608 | tf_op jit(solution)/shard_map/slice | solution.py:130
  136.7 3.0 reshape.207
  139.7 4.2 %reshape.208 = f32[8,8,2,4096]{3,2,0,1:T(2,128)} reshape(f32[1,8,8,8192]{3,1,2,0:T(8,128)} %get-tuple-element.12) | data formatting | bytes 4194304 | tf_op jit(solution)/shard_map/squeeze | solution.py:130
  143.9 5.8 %subtract_reduce_fusion.1 = (f32[8,8,4096]{2,1,0:T(8,128)S(1)}, f32[8,8,4096]{2,1,0:T(8,128)S(1)}) fusion(f32[8,8,2,4096]{3,2,0,1:T(2,128)} %reshape.208, f32[8,8,2,4096]{3,2,0,1:T(2,128)S(1)} %reshape.207, f32[2]{0:T(128)S(1)} %get-tuple-element.30, f32[2]{0:T(128)S(1)} %get-tuple-element.29), kind=kLoop, calls=%fused_computation.35 | loop fusion | flops 3670016 | bytes 6291472 | tf_op jit(solution)/shard_map/reduce_sum | solution.py:130
  149.7 0.6 copy.185
  150.3 0.6 copy.186
  150.9 1.5 fusion.99
  152.4 1.5 fusion.100
  153.9 1.5 fusion.3
  155.4 1.5 fusion.2
  156.9 1.6 fusion.87
  158.6 1.2 fusion.86
  159.8 1.2 convolution_subtract_fusion.2
  161.1 1.2 convolution_add_fusion.2
  162.3 1.2 fusion.89
  163.5 1.2 fusion.88
  164.8 1.2 convolution_subtract_fusion.1
  166.0 1.2 convolution_add_fusion.1
  167.2 1.2 fusion.90
  168.4 1.4 fusion.91
  169.8 2.2 fusion.1
  172.0 2.4 reshape.194
  174.4 2.2 fusion
  176.5 1.5 reshape.195
  178.1 1.6 multiply_subtract_fusion
  179.7 0.7 all-gather.8.cloned.1.call-update
  180.5 32.5 %all-gather.6.cloned.1.call-done = f32[8,8,8192]{2,1,0:T(8,128)} async-done(((f32[8,8,4096]{2,1,0:T(8,128)}), f32[8,8,8192]{2,1,0:T(8,128)}) %all-gather.6.cloned.1.call-update) | async-done | bytes 2097168 | tf_op jit(solution)/shard_map/all_gather | solution.py:148
  212.9 34.7 %all-gather.8.cloned.1.call-done = f32[8,8,8192]{2,1,0:T(8,128)} async-done(((f32[8,8,4096]{2,1,0:T(8,128)}), f32[8,8,8192]{2,1,0:T(8,128)}) %all-gather.8.cloned.1.call-update) | async-done | bytes 2097168 | tf_op jit(solution)/shard_map/all_gather | solution.py:149
  247.6 3.2 subtract_reduce_fusion
  250.8 0.6 fusion.74
  251.4 0.6 fusion.75
  252.0 0.1 fusion.95
  252.1 0.1 pad_maximum_fusion.2
  252.2 0.6 copy.118
  252.8 17.0 %all_to_all.57 = bf16[4,2,8,8,1024]{4,3,2,1,0:T(8,128)(2,1)S(1)} all-to-all(bf16[4,2,8,8,1024]{4,3,2,1,0:T(8,128)(2,1)S(1)} %copy.118), channel_id=1, replica_groups=mesh['chan'=4,'pulse'=4,'range'=2] {'pulse'}, dimensions={0} | all-to-all | bytes 2097152 | tf_op jit(solution)/shard_map/all_to_all | solution.py:169
  269.9 0.4 fusion.79
  270.2 0.4 fusion.77
  270.6 0.4 fusion.7
  271.0 0.4 fusion.6
  271.4 0.6 copy.121
  272.0 16.9 %all_to_all.58 = f32[8,32,1024]{2,0,1:T(8,128)S(1)} all-to-all(f32[8,32,1024]{2,0,1:T(8,128)S(1)} %copy.121), channel_id=1, replica_groups=mesh['chan'=4,'pulse'=4,'range'=2] {'pulse'}, dimensions={1} | all-to-all | bytes 2097152 | tf_op jit(solution)/shard_map/all_to_all | solution.py:177
  288.8 0.6 copy.122
  289.5 2.4 collective-permute-start
  291.9 1.3 collective-permute-start.1
  293.2 0.3 collective-permute-done
  293.5 4.2 %collective-permute-done.1 = f32[8,8,20]{2,1,0:T(8,128)S(1)} collective-permute-done((f32[8,8,20]{2,1,0:T(8,128)S(1)}, f32[8,8,20]{2,1,0:T(8,128)S(1)}, u32[]{:S(2)}, u32[]{:S(2)}) %collective-permute-start.1) | collective-permute-done | bytes 5152 | tf_op jit(solution)/shard_map/ppermute | solution.py:21
  297.7 12.2 %fusion.14 = f32[8,8,4096]{2,1,0:T(8,128)} fusion(f32[8,8,4096]{2,1,0:T(8,128)S(1)} %bitcast.152, f32[8,8,20]{2,1,0:T(8,128)S(1)} %collective-permute-done.1, f32[8,8,20]{2,1,0:T(8,128)S(1)} %collective-permute-done), kind=kLoop, calls=%fused_computation.66 | loop fusion | flops 17301504 | bytes 2107392 | tf_op jit(solution)/shard_map/div | solution.py:196
  (22 shorter events, 0.8 us)
Async XLA Ops:
  10.6 6.5 %copy-start.2 = (bf16[2,32,64]{2,1,0:T(8,128)(2,1)S(1)}, bf16[2,32,64]{2,1,0:T(8,128)(2,1)}, u32[]{:S(2)}) copy-start(bf16[2,32,64]{2,1,0:T(8,128)(2,1)} %param.4) | copy-start | bytes 24580
  10.6 54.7 %all-to-all-start = ((bf16[2,16,8,4096]{3,1,0,2:T(8,128)(2,1)}), bf16[2,16,8,4096]{3,1,0,2:T(8,128)(2,1)S(1)}, u32[]{:S(2)}, u32[]{:S(2)}) async-start(bf16[2,16,8,4096]{3,1,0,2:T(8,128)(2,1)} %copy.93), calls=%async_computation | async-start | bytes 4194304 | tf_op jit(solution)/shard_map/all_to_all | solution.py:107
  17.1 115.6 %all-gather.4.cloned.1.call-start = ((), (), s32[]{:S(2)}) async-start(), calls=%async_computation.4 | async-start | bytes 3145728 | tf_op jit(solution)/shard_map/all_gather | solution.py:119
  99.3 1.3 copy-start.1
  100.4 112.6 %all-gather.6.cloned.1.call-start = ((), (), s32[]{:S(2)}) async-start(), calls=%async_computation.5 | async-start | bytes 3145728 | tf_op jit(solution)/shard_map/all_gather | solution.py:148
  176.5 1.5 copy-start
  179.7 67.9 %all-gather.8.cloned.1.call-start = ((), (), s32[]{:S(2)}) async-start(), calls=%async_computation.6 | async-start | bytes 3145728 | tf_op jit(solution)/shard_map/all_gather | solution.py:149
  289.5 4.0 %collective-permute-start = (f32[8,8,20]{2,1,0:T(8,128)S(1)}, f32[8,8,20]{2,1,0:T(8,128)S(1)}, u32[]{:S(2)}, u32[]{:S(2)}) collective-permute-start(f32[8,8,20]{2,1,0:T(8,128)S(1)} %get-tuple-element.13), channel_id=1, source_target_pairs={{0,1},{2,3},{4,5},{6,7},{8,9},{10,11},{12,13},{14,15},{16,17},{18,... | collective-permute-start | bytes 15368 | tf_op jit(solution)/shard_map/ppermute | solution.py:20
  291.9 5.8 %collective-permute-start.1 = (f32[8,8,20]{2,1,0:T(8,128)S(1)}, f32[8,8,20]{2,1,0:T(8,128)S(1)}, u32[]{:S(2)}, u32[]{:S(2)}) collective-permute-start(f32[8,8,20]{2,1,0:T(8,128)S(1)} %get-tuple-element.14), channel_id=1, source_target_pairs={{1,0},{3,2},{5,4},{7,6},{9,8},{11,10},{13,12},{15,14},{17,16},{19,... | collective-permute-start | bytes 15368 | tf_op jit(solution)/shard_map/ppermute | solution.py:21
Sparse Core Ops, SparseCore 0:
  100.5 32.1 all-gather.3
  179.8 33.0 all-gather.5
  214.5 33.0 all-gather.7
